TPU v7x, 256 devices: a whole 4x4x8 slice. The times are simulated.
256 devices in a mesh: inst: 4 (over y_hi, core), cells: 64 (over y_lo, x, z).
Axes of the slice: x: 4, y: 4 (y_hi: 2, y_lo: 2; y = y_hi * 2 + y_lo), z: 8, core: 2. Of those that a mesh axis runs over, the one named last changes fastest.
Arguments:
- flow_state: float32 [8, 5, 512, 32, 128], P('inst', None, 'cells'), may hold values from -6 to 6
- forcing: float32 [8, 5, 512, 32, 128], P('inst', None, 'cells'), may hold values from -6 to 6
- diffusion: float32 [512, 32, 128], P('cells'), may hold values from 0.2 to 0.6
- block_inverse: float32 [5, 5, 512, 32, 128], P(None, None, 'cells', 'inst'), may hold values from -0.03 to 0.15, as said below
Outputs:
- new_state: float32 [8, 5, 512, 32, 128], P('inst', None, 'cells')
Inputs may be any that keep to these rules, and one draw needn't show every extreme that they name: block_inverse[v, v] lies between 0.06 and 0.15; entries off the diagonal lie between -0.03 and 0.03.
All inputs are finite; a program needn't handle non-finite values.
Results may differ from a plain program's by a relative error of at most 0.0001.
Values sent between devices are 32-bit elements; how exact they have to be, the bound alone decides.
A program may use at most 64 MiB of HBM per device.

v0:
```python
import math

import jax
import jax.numpy as jnp
from jax import lax
from jax.sharding import PartitionSpec as P

SWEEPS = 4


frequency = 1.0


def extended(shard, sides, width):
    edges = {}
    for axis, dim in sides:
        size, length = (lax.axis_size(axis), shard.shape[dim])
        up = [(i, (i + 1) % size) for i in range(size - 1)]
        last = lax.slice_in_dim(shard, length - width, length, axis=dim)
        initial = lax.slice_in_dim(shard, 0, width, axis=dim)
        edges[dim] = (
            lax.ppermute(last, axis, up),
            lax.ppermute(initial, axis, [(b, a) for a, b in up]),
        )
    done = []
    for _, dim in sides:
        low, high = edges[dim]
        around = [(width, width) if d in done else (0, 0) for d in range(shard.ndim)]
        shard = jnp.concatenate([jnp.pad(low, around), shard, jnp.pad(high, around)], axis=dim)
        done.append(dim)
    return shard


def extended_2(shard, sides, width):
    for axis, dim in sides:
        size, length = (lax.axis_size(axis), shard.shape[dim])
        up = [(i, (i + 1) % size) for i in range(size - 1)]
        down = [(j, i) for i, j in up]
        last = lax.slice_in_dim(shard, length - width, length, axis=dim)
        initial = lax.slice_in_dim(shard, 0, width, axis=dim)
        before = lax.ppermute(last, axis, up)
        after = lax.ppermute(initial, axis, down)
        shard = jnp.concatenate([before, shard, after], axis=dim)
    return shard


def spectral_matrix(count):
    index = jnp.arange(count)
    offset = index[:, None] - index[None, :]
    parity = jnp.where(offset % 2 == 0, 1.0, -1.0)
    angle = math.pi * jnp.where(offset == 0, 1, offset) / count
    entries = 0.5 * parity / jnp.tan(angle)
    return jnp.where(offset == 0, 0.0, entries).astype(jnp.float32)


def interior_sum(padded):
    padded = jnp.pad(padded, ((0, 0), (0, 0), (0, 0), (0, 0), (1, 1)))
    beside = padded[:, :, 2:, 1:-1, 1:-1] + padded[:, :, :-2, 1:-1, 1:-1]
    beside = beside + padded[:, :, 1:-1, 2:, 1:-1] + padded[:, :, 1:-1, :-2, 1:-1]
    beside = beside + padded[:, :, 1:-1, 1:-1, 2:] + padded[:, :, 1:-1, 1:-1, :-2]
    return beside


def block_neighbours(grid_field):
    padded = extended(grid_field, (("inst", 3), ("cells", 2)), 1)
    return interior_sum(padded)


def spectral_term(matrix, grid_field):
    flat = grid_field.reshape(grid_field.shape[0], -1)
    product = jnp.dot(matrix, flat, precision=lax.Precision.HIGHEST)
    return (frequency * product).reshape(grid_field.shape)


def apply_blocks(block_inverse, source):
    outputs = []
    for row_index in range(block_inverse.shape[0]):
        total = block_inverse[row_index, 0][None] * source[:, 0]
        for col_index in range(1, block_inverse.shape[1]):
            total = total + block_inverse[row_index, col_index][None] * source[:, col_index]
        outputs.append(total)
    return jnp.stack(outputs, axis=1)


def on_device(flow_state, forcing, diffusion, block_inverse):
    block_rows = block_inverse.shape[3]
    first_row = lax.axis_index("inst") * block_rows
    weight_block = lax.dynamic_slice_in_dim(diffusion, first_row, block_rows, 1)[None, None]
    matrix = spectral_matrix(lax.axis_size("inst") * flow_state.shape[0])
    padded = extended_2(flow_state, (("cells", 2),), 1)
    padded = jnp.pad(padded, ((0, 0), (0, 0), (0, 0), (1, 1), (0, 0)))
    local_part = diffusion[None, None] * (6.0 * flow_state - interior_sum(padded)) - forcing
    moved_state, moved_part = (
        lax.all_to_all(flow_state, "inst", split_axis=3, concat_axis=0, tiled=True),
        lax.all_to_all(local_part, "inst", split_axis=3, concat_axis=0, tiled=True),
    )
    residual = moved_part + spectral_term(matrix, moved_state)
    update = apply_blocks(block_inverse, -residual)
    for sweep_index in range(SWEEPS):
        source = -residual - spectral_term(matrix, update) + weight_block * block_neighbours(update)
        update = apply_blocks(block_inverse, source)
    return lax.all_to_all(moved_state + update, "inst", split_axis=0, concat_axis=3, tiled=True)


def solution(mesh):
    in_specs = (
        P("inst", None, "cells", None, None),
        P("inst", None, "cells", None, None),
        P("cells", None, None),
        P(None, None, "cells", "inst", None),
    )
    out_specs = P("inst", None, "cells", None, None)
    return jax.shard_map(
        on_device, mesh=mesh, in_specs=in_specs, out_specs=out_specs, check_vma=False
    )
```

profile of v0, /device:TPU:24, one launch (start us, length us, event | category | flops | bytes accessed | tf_op | source)
XLA Modules:
  0.0 188.6 jit_solution(16845610435672489864)
XLA Ops:
  0.0 3.1 %copy.21 = f32[2,5,8,32,128]{4,2,1,0,3:T(8,128)} copy(f32[2,5,8,32,128]{4,3,2,1,0:T(8,128)} %param.4) | data formatting | bytes 2621440 | tf_op args[0]
  3.1 4.9 %all-to-all-start = ((f32[2,5,8,32,128]{4,2,1,0,3:T(8,128)}), f32[2,5,8,32,128]{4,2,1,0,3:T(8,128)S(1)}, u32[]{:S(2)}, u32[]{:S(2)}) async-start(f32[2,5,8,32,128]{4,2,1,0,3:T(8,128)} %copy.21), calls=%async_computation | async-start | bytes 2621440 | tf_op jit(solution)/shard_map/all_to_all | solution.py:94
  9.1 3.8 %collective-permute-start.1 = (f32[2,5,1,32,128]{4,3,2,1,0:T(8,128)S(1)}, f32[2,5,1,32,128]{4,3,2,1,0:T(8,128)S(1)}, u32[]{:S(2)}, u32[]{:S(2)}) collective-permute-start(f32[2,5,1,32,128]{4,3,2,1,0:T(8,128)S(1)} %get-tuple-element.21), channel_id=1, source_target_pairs={{0,1},{1,2},{2,3},{3,4},{4,5},{5,6},{6,7},{7,8},{8,9},{9,10},{10,1... | collective-permute-start | bytes 491528 | tf_op jit(solution)/shard_map/ppermute | solution.py:41
  12.9 8.2 %collective-permute-start = (f32[2,5,1,32,128]{4,3,2,1,0:T(8,128)S(1)}, f32[2,5,1,32,128]{4,3,2,1,0:T(8,128)S(1)}, u32[]{:S(2)}, u32[]{:S(2)}) collective-permute-start(f32[2,5,1,32,128]{4,3,2,1,0:T(8,128)S(1)} %get-tuple-element.22), channel_id=1, source_target_pairs={{1,0},{2,1},{3,2},{4,3},{5,4},{6,5},{7,6},{8,7},{9,8},{10,9},{11,1... | collective-permute-start | bytes 491528 | tf_op jit(solution)/shard_map/ppermute | solution.py:42
  21.3 2.5 %collective-permute-done.1 = f32[2,5,1,32,128]{4,3,2,1,0:T(8,128)S(1)} collective-permute-done((f32[2,5,1,32,128]{4,3,2,1,0:T(8,128)S(1)}, f32[2,5,1,32,128]{4,3,2,1,0:T(8,128)S(1)}, u32[]{:S(2)}, u32[]{:S(2)}) %collective-permute-start.1) | collective-permute-done | bytes 163872 | tf_op jit(solution)/shard_map/ppermute | solution.py:41
  27.0 5.4 %fusion.7 = f32[2,5,8,32,128]{4,2,1,0,3:T(8,128)} fusion(f32[2,5,10,34,128]{4,2,1,0,3:T(8,128)S(1)} %select_maximum_fusion.16, f32[2,5,8,32,128]{4,2,1,0,3:T(8,128)} %copy.21, f32[2,5,1,32,128]{4,2,1,0,3:T(1,128)S(1)} %copy.27, f32[2,5,1,32,128]{4,2,1,0,3:T(1,128)S(1)} %copy.26, f32[2,5,8,32,128]{4,3,2,1,0:T(8,128)S(1)} %copy-done.2, f32[8,32,128]{2,0,1:T(8,128)S(1)} %copy.23), kind=kLoop, calls=%fused_computation.36 | loop fusion | flops 3604480 | bytes 9797632 | tf_op jit(solution)/shard_map/sub | solution.py:92
  32.4 5.4 %all-to-all-start.1 = ((f32[2,5,8,32,128]{4,2,1,0,3:T(8,128)}), f32[2,5,8,32,128]{4,2,1,0,3:T(8,128)}, u32[]{:S(2)}, u32[]{:S(2)}) async-start(f32[2,5,8,32,128]{4,2,1,0,3:T(8,128)} %fusion.7), calls=%async_computation.1 | async-start | bytes 2621440 | tf_op jit(solution)/shard_map/all_to_all | solution.py:95
  38.6 14.9 %all-to-all-done.1 = f32[2,5,8,32,128]{4,2,1,0,3:T(8,128)} async-done(((f32[2,5,8,32,128]{4,2,1,0,3:T(8,128)}), f32[2,5,8,32,128]{4,2,1,0,3:T(8,128)}, u32[]{:S(2)}, u32[]{:S(2)}) %all-to-all-start.1) | async-done | bytes 1310752 | tf_op jit(solution)/shard_map/all_to_all | solution.py:95
  53.5 2.0 %copy.33 = f32[2,5,8,4,8,128]{5,0,3,4,2,1:T(2,128)S(1)} copy(f32[2,5,8,4,8,128]{5,2,1,0,4,3:T(8,128)} %bitcast.4) | data formatting | bytes 2621440 | tf_op jit(solution)/shard_map/all_to_all | solution.py:95
  61.4 8.3 %collective-permute-start.4 = (f32[8,5,1,8,128]{4,0,3,2,1:T(8,128)}, f32[8,5,1,8,128]{4,0,3,2,1:T(8,128)}, u32[]{:S(2)}, u32[]{:S(2)}) collective-permute-start(f32[8,5,1,8,128]{4,0,3,2,1:T(8,128)} %get-tuple-element.20), channel_id=1, source_target_pairs={{1,0},{2,1},{3,2},{4,3},{5,4},{6,5},{7,6},{8,7},{9,8},{10,9},{11,1... | collective-permute-start | bytes 491528 | tf_op jit(solution)/shard_map/ppermute | solution.py:23
  69.7 1.9 %collective-permute-start.2 = (f32[8,5,8,1,128]{4,0,3,2,1:T(8,128)}, f32[8,5,8,1,128]{4,0,3,2,1:T(8,128)}, u32[]{:S(2)}, u32[]{:S(2)}) collective-permute-start(f32[8,5,8,1,128]{4,0,3,2,1:T(8,128)} %get-tuple-element.17), channel_id=1, source_target_pairs={{0,64},{64,128},{128,192},{1,65},{65,129},{129,193},{2,66},{66,130... | collective-permute-start | bytes 491528 | tf_op jit(solution)/shard_map/ppermute | solution.py:22
  71.6 5.3 %collective-permute-start.3 = (f32[8,5,8,1,128]{4,0,3,2,1:T(8,128)}, f32[8,5,8,1,128]{4,0,3,2,1:T(8,128)}, u32[]{:S(2)}, u32[]{:S(2)}) collective-permute-start(f32[8,5,8,1,128]{4,0,3,2,1:T(8,128)} %get-tuple-element.18), channel_id=1, source_target_pairs={{64,0},{128,64},{192,128},{65,1},{129,65},{193,129},{66,2},{130,66... | collective-permute-start | bytes 491528 | tf_op jit(solution)/shard_map/ppermute | solution.py:23
  79.9 4.4 %select_maximum_fusion.12 = f32[8,5,10,10,130]{4,0,3,2,1:T(8,128)S(1)} fusion(f32[8,5,1,10,128]{4,0,3,2,1:T(8,128)S(1)} %pad.48, f32[8,5,1,10,128]{4,0,3,2,1:T(8,128)S(1)} %pad.49, f32[8,5,8,1,128]{4,0,3,2,1:T(8,128)} %collective-permute-done.3, f32[8,5,8,8,128]{4,0,3,2,1:T(8,128)} %copy-done, f32[8,5,8,1,128]{4,0,3,2,1:T(8,128)} %collective-permute-done.2), kind=kLoop, calls=%fused_computation.18 | loop fusion | flops 6240000 | bytes 4128000 | tf_op jit(solution)/shard_map/concatenate | solution.py:29
  84.3 3.5 %fusion.24 = f32[8,5,8,8,128]{4,0,3,2,1:T(8,128)S(1)} fusion(f32[8,5,10,10,130]{4,0,3,2,1:T(8,128)S(1)} %select_maximum_fusion.12, f32[8,5,8,8,128]{4,0,3,2,1:T(8,128)S(1)} %copy-done.1, f32[8,5,8,1,128]{4,0,3,2,1:T(8,128)} %collective-permute-done.2, f32[8,5,8,1,128]{4,0,3,2,1:T(8,128)} %collective-permute-done.3, f32[8,5,1,10,128]{4,0,3,2,1:T(8,128)S(1)} %pad.49, ...), kind=kOutput, calls=%fused_computation.84 | convolution fusion | flops 36701504 | bytes 8634368 | tf_op jit(solution)/shard_map/dot_general | solution.py:71
  88.9 1.9 %collective-permute-start.9 = (f32[8,5,1,8,128]{4,0,3,2,1:T(8,128)S(1)}, f32[8,5,1,8,128]{4,0,3,2,1:T(8,128)S(1)}, u32[]{:S(2)}, u32[]{:S(2)}) collective-permute-start(f32[8,5,1,8,128]{4,0,3,2,1:T(8,128)S(1)} %get-tuple-element.15), channel_id=1, source_target_pairs={{0,1},{1,2},{2,3},{3,4},{4,5},{5,6},{6,7},{7,8},{8,9},{9,10},{10,1... | collective-permute-start | bytes 491528 | tf_op jit(solution)/shard_map/ppermute | solution.py:22
  90.8 8.1 %collective-permute-start.8 = (f32[8,5,1,8,128]{4,0,3,2,1:T(8,128)S(1)}, f32[8,5,1,8,128]{4,0,3,2,1:T(8,128)S(1)}, u32[]{:S(2)}, u32[]{:S(2)}) collective-permute-start(f32[8,5,1,8,128]{4,0,3,2,1:T(8,128)S(1)} %get-tuple-element.16), channel_id=1, source_target_pairs={{1,0},{2,1},{3,2},{4,3},{5,4},{6,5},{7,6},{8,7},{9,8},{10,9},{11,1... | collective-permute-start | bytes 491528 | tf_op jit(solution)/shard_map/ppermute | solution.py:23
  99.0 1.9 %collective-permute-start.6 = (f32[8,5,8,1,128]{4,0,3,2,1:T(8,128)S(1)}, f32[8,5,8,1,128]{4,0,3,2,1:T(8,128)S(1)}, u32[]{:S(2)}, u32[]{:S(2)}) collective-permute-start(f32[8,5,8,1,128]{4,0,3,2,1:T(8,128)S(1)} %get-tuple-element.13), channel_id=1, source_target_pairs={{0,64},{64,128},{128,192},{1,65},{65,129},{129,193},{2,66},{66,130... | collective-permute-start | bytes 491528 | tf_op jit(solution)/shard_map/ppermute | solution.py:22
  100.9 5.1 %collective-permute-start.7 = (f32[8,5,8,1,128]{4,0,3,2,1:T(8,128)S(1)}, f32[8,5,8,1,128]{4,0,3,2,1:T(8,128)S(1)}, u32[]{:S(2)}, u32[]{:S(2)}) collective-permute-start(f32[8,5,8,1,128]{4,0,3,2,1:T(8,128)S(1)} %get-tuple-element.14), channel_id=1, source_target_pairs={{64,0},{128,64},{192,128},{65,1},{129,65},{193,129},{66,2},{130,66... | collective-permute-start | bytes 491528 | tf_op jit(solution)/shard_map/ppermute | solution.py:23
  108.9 2.8 %select_maximum_fusion.8 = f32[8,5,10,10,130]{4,0,3,2,1:T(8,128)S(1)} fusion(f32[8,5,1,10,128]{4,0,3,2,1:T(8,128)S(1)} %pad.51, f32[8,5,1,10,128]{4,0,3,2,1:T(8,128)S(1)} %pad.52, f32[8,5,8,1,128]{4,0,3,2,1:T(8,128)S(1)} %collective-permute-done.7, f32[8,5,8,8,128]{4,0,3,2,1:T(8,128)S(1)} %add_dynamic-update-slice_fusion.15, ...), kind=kLoop, calls=%fused_computation.14 | loop fusion | flops 6240000 | bytes 4128000 | tf_op jit(solution)/shard_map/concatenate | solution.py:29
  111.7 2.0 %fusion.19 = f32[8,5,8,8,128]{4,0,3,2,1:T(8,128)S(1)} fusion(f32[8,5,10,10,130]{4,0,3,2,1:T(8,128)S(1)} %select_maximum_fusion.8, f32[8,5,8,8,128]{4,0,3,2,1:T(8,128)S(1)} %add_dynamic-update-slice_fusion.15, f32[8,5,8,1,128]{4,0,3,2,1:T(8,128)S(1)} %collective-permute-done.6, f32[8,5,8,1,128]{4,0,3,2,1:T(8,128)S(1)} %collective-permute-done.7, ...), kind=kOutput, calls=%fused_computation.69 | convolution fusion | flops 36701504 | bytes 8634368 | tf_op jit(solution)/shard_map/dot_general | solution.py:71
  114.8 1.9 %collective-permute-start.13 = (f32[8,5,1,8,128]{4,0,3,2,1:T(8,128)S(1)}, f32[8,5,1,8,128]{4,0,3,2,1:T(8,128)S(1)}, u32[]{:S(2)}, u32[]{:S(2)}) collective-permute-start(f32[8,5,1,8,128]{4,0,3,2,1:T(8,128)S(1)} %get-tuple-element.11), channel_id=1, source_target_pairs={{0,1},{1,2},{2,3},{3,4},{4,5},{5,6},{6,7},{7,8},{8,9},{9,10},{10,1... | collective-permute-start | bytes 491528 | tf_op jit(solution)/shard_map/ppermute | solution.py:22
  116.7 8.1 %collective-permute-start.12 = (f32[8,5,1,8,128]{4,0,3,2,1:T(8,128)S(1)}, f32[8,5,1,8,128]{4,0,3,2,1:T(8,128)S(1)}, u32[]{:S(2)}, u32[]{:S(2)}) collective-permute-start(f32[8,5,1,8,128]{4,0,3,2,1:T(8,128)S(1)} %get-tuple-element.12), channel_id=1, source_target_pairs={{1,0},{2,1},{3,2},{4,3},{5,4},{6,5},{7,6},{8,7},{9,8},{10,9},{11,1... | collective-permute-start | bytes 491528 | tf_op jit(solution)/shard_map/ppermute | solution.py:23
  124.9 1.9 %collective-permute-start.10 = (f32[8,5,8,1,128]{4,0,3,2,1:T(8,128)S(1)}, f32[8,5,8,1,128]{4,0,3,2,1:T(8,128)S(1)}, u32[]{:S(2)}, u32[]{:S(2)}) collective-permute-start(f32[8,5,8,1,128]{4,0,3,2,1:T(8,128)S(1)} %get-tuple-element.9), channel_id=1, source_target_pairs={{0,64},{64,128},{128,192},{1,65},{65,129},{129,193},{2,66},{66,130... | collective-permute-start | bytes 491528 | tf_op jit(solution)/shard_map/ppermute | solution.py:22
  126.8 5.4 %collective-permute-start.11 = (f32[8,5,8,1,128]{4,0,3,2,1:T(8,128)S(1)}, f32[8,5,8,1,128]{4,0,3,2,1:T(8,128)S(1)}, u32[]{:S(2)}, u32[]{:S(2)}) collective-permute-start(f32[8,5,8,1,128]{4,0,3,2,1:T(8,128)S(1)} %get-tuple-element.10), channel_id=1, source_target_pairs={{64,0},{128,64},{192,128},{65,1},{129,65},{193,129},{66,2},{130,66... | collective-permute-start | bytes 491528 | tf_op jit(solution)/shard_map/ppermute | solution.py:23
  134.8 2.8 %select_maximum_fusion.4 = f32[8,5,10,10,130]{4,0,3,2,1:T(8,128)S(1)} fusion(f32[8,5,1,10,128]{4,0,3,2,1:T(8,128)S(1)} %pad.54, f32[8,5,1,10,128]{4,0,3,2,1:T(8,128)S(1)} %pad.55, f32[8,5,8,1,128]{4,0,3,2,1:T(8,128)S(1)} %collective-permute-done.11, f32[8,5,8,8,128]{4,0,3,2,1:T(8,128)S(1)} %add_dynamic-update-slice_fusion.10, ...), kind=kLoop, calls=%fused_computation.10 | loop fusion | flops 6240000 | bytes 4128000 | tf_op jit(solution)/shard_map/concatenate | solution.py:29
  137.6 2.0 %fusion.14 = f32[8,5,8,8,128]{4,0,3,2,1:T(8,128)S(1)} fusion(f32[8,5,10,10,130]{4,0,3,2,1:T(8,128)S(1)} %select_maximum_fusion.4, f32[8,5,8,8,128]{4,0,3,2,1:T(8,128)S(1)} %add_dynamic-update-slice_fusion.10, f32[8,5,8,1,128]{4,0,3,2,1:T(8,128)S(1)} %collective-permute-done.10, f32[8,5,8,1,128]{4,0,3,2,1:T(8,128)S(1)} %collective-permute-done.11, ...), kind=kOutput, calls=%fused_computation.54 | convolution fusion | flops 36701504 | bytes 8634368 | tf_op jit(solution)/shard_map/dot_general | solution.py:71
  140.7 1.9 %collective-permute-start.17 = (f32[8,5,1,8,128]{4,0,3,2,1:T(8,128)S(1)}, f32[8,5,1,8,128]{4,0,3,2,1:T(8,128)S(1)}, u32[]{:S(2)}, u32[]{:S(2)}) collective-permute-start(f32[8,5,1,8,128]{4,0,3,2,1:T(8,128)S(1)} %get-tuple-element.7), channel_id=1, source_target_pairs={{0,1},{1,2},{2,3},{3,4},{4,5},{5,6},{6,7},{7,8},{8,9},{9,10},{10,1... | collective-permute-start | bytes 491528 | tf_op jit(solution)/shard_map/ppermute | solution.py:22
  142.6 8.1 %collective-permute-start.16 = (f32[8,5,1,8,128]{4,0,3,2,1:T(8,128)S(1)}, f32[8,5,1,8,128]{4,0,3,2,1:T(8,128)S(1)}, u32[]{:S(2)}, u32[]{:S(2)}) collective-permute-start(f32[8,5,1,8,128]{4,0,3,2,1:T(8,128)S(1)} %get-tuple-element.8), channel_id=1, source_target_pairs={{1,0},{2,1},{3,2},{4,3},{5,4},{6,5},{7,6},{8,7},{9,8},{10,9},{11,1... | collective-permute-start | bytes 491528 | tf_op jit(solution)/shard_map/ppermute | solution.py:23
  152.7 5.1 %collective-permute-start.15 = (f32[8,5,8,1,128]{4,0,3,2,1:T(8,128)S(1)}, f32[8,5,8,1,128]{4,0,3,2,1:T(8,128)S(1)}, u32[]{:S(2)}, u32[]{:S(2)}) collective-permute-start(f32[8,5,8,1,128]{4,0,3,2,1:T(8,128)S(1)} %get-tuple-element.6), channel_id=1, source_target_pairs={{64,0},{128,64},{192,128},{65,1},{129,65},{193,129},{66,2},{130,66... | collective-permute-start | bytes 491528 | tf_op jit(solution)/shard_map/ppermute | solution.py:23
  160.7 2.8 %select_maximum_fusion = f32[8,5,10,10,130]{4,0,3,2,1:T(8,128)S(1)} fusion(f32[8,5,1,10,128]{4,0,3,2,1:T(8,128)S(1)} %pad.57, f32[8,5,1,10,128]{4,0,3,2,1:T(8,128)S(1)} %pad.58, f32[8,5,8,1,128]{4,0,3,2,1:T(8,128)S(1)} %collective-permute-done.15, f32[8,5,8,8,128]{4,0,3,2,1:T(8,128)S(1)} %add_dynamic-update-slice_fusion.5, ...), kind=kLoop, calls=%fused_computation.6 | loop fusion | flops 6240000 | bytes 4128000 | tf_op jit(solution)/shard_map/concatenate | solution.py:29
  163.5 2.0 %fusion.9 = f32[8,5,8,8,128]{4,0,3,2,1:T(8,128)S(1)} fusion(f32[8,5,10,10,130]{4,0,3,2,1:T(8,128)S(1)} %select_maximum_fusion, f32[8,5,8,8,128]{4,0,3,2,1:T(8,128)S(1)} %add_dynamic-update-slice_fusion.5, f32[8,5,8,1,128]{4,0,3,2,1:T(8,128)S(1)} %collective-permute-done.14, f32[8,5,8,1,128]{4,0,3,2,1:T(8,128)S(1)} %collective-permute-done.15, ...), kind=kOutput, calls=%fused_computation.39 | convolution fusion | flops 36701504 | bytes 8634368 | tf_op jit(solution)/shard_map/dot_general | solution.py:71
  167.1 20.3 %all_to_all.54 = f32[8,5,8,8,128]{4,3,2,1,0:T(8,128)S(1)} all-to-all(f32[8,5,8,8,128]{4,3,2,1,0:T(8,128)S(1)} %copy.34), channel_id=1, replica_groups=mesh['inst'=4,'cells'=64] {'inst'}, dimensions={0} | all-to-all | bytes 2621440 | tf_op jit(solution)/shard_map/all_to_all | solution.py:102
  (84 shorter events, 29.7 us)
Async XLA Ops:
  3.1 18.0 %copy-start.4 = (f32[8,32,128]{2,1,0:T(8,128)S(1)}, f32[8,32,128]{2,1,0:T(8,128)}, u32[]{:S(2)}) copy-start(f32[8,32,128]{2,1,0:T(8,128)} %param.6) | copy-start | bytes 393220
  3.1 29.3 %all-to-all-start = ((f32[2,5,8,32,128]{4,2,1,0,3:T(8,128)}), f32[2,5,8,32,128]{4,2,1,0,3:T(8,128)S(1)}, u32[]{:S(2)}, u32[]{:S(2)}) async-start(f32[2,5,8,32,128]{4,2,1,0,3:T(8,128)} %copy.21), calls=%async_computation | async-start | bytes 2621440 | tf_op jit(solution)/shard_map/all_to_all | solution.py:94
  9.1 14.7 %collective-permute-start.1 = (f32[2,5,1,32,128]{4,3,2,1,0:T(8,128)S(1)}, f32[2,5,1,32,128]{4,3,2,1,0:T(8,128)S(1)}, u32[]{:S(2)}, u32[]{:S(2)}) collective-permute-start(f32[2,5,1,32,128]{4,3,2,1,0:T(8,128)S(1)} %get-tuple-element.21), channel_id=1, source_target_pairs={{0,1},{1,2},{2,3},{3,4},{4,5},{5,6},{6,7},{7,8},{8,9},{9,10},{10,1... | collective-permute-start | bytes 491528 | tf_op jit(solution)/shard_map/ppermute | solution.py:41
  12.9 12.0 %collective-permute-start = (f32[2,5,1,32,128]{4,3,2,1,0:T(8,128)S(1)}, f32[2,5,1,32,128]{4,3,2,1,0:T(8,128)S(1)}, u32[]{:S(2)}, u32[]{:S(2)}) collective-permute-start(f32[2,5,1,32,128]{4,3,2,1,0:T(8,128)S(1)} %get-tuple-element.22), channel_id=1, source_target_pairs={{1,0},{2,1},{3,2},{4,3},{5,4},{6,5},{7,6},{8,7},{9,8},{10,9},{11,1... | collective-permute-start | bytes 491528 | tf_op jit(solution)/shard_map/ppermute | solution.py:42
  25.1 1.9 %copy-start.2 = (f32[2,5,8,32,128]{4,3,2,1,0:T(8,128)S(1)}, f32[2,5,8,32,128]{4,3,2,1,0:T(8,128)}, u32[]{:S(2)}) copy-start(f32[2,5,8,32,128]{4,3,2,1,0:T(8,128)} %param.5) | copy-start | bytes 3932164
  32.4 5.4 %copy-start.3 = (f32[5,5,8,8,128]{4,3,2,1,0:T(8,128)S(1)}, f32[5,5,8,8,128]{4,3,2,1,0:T(8,128)}, u32[]{:S(2)}) copy-start(f32[5,5,8,8,128]{4,3,2,1,0:T(8,128)} %param.7) | copy-start | bytes 2457604
  32.4 21.1 %all-to-all-start.1 = ((f32[2,5,8,32,128]{4,2,1,0,3:T(8,128)}), f32[2,5,8,32,128]{4,2,1,0,3:T(8,128)}, u32[]{:S(2)}, u32[]{:S(2)}) async-start(f32[2,5,8,32,128]{4,2,1,0,3:T(8,128)} %fusion.7), calls=%async_computation.1 | async-start | bytes 2621440 | tf_op jit(solution)/shard_map/all_to_all | solution.py:95
  57.6 1.2 copy-start
  59.5 18.2 %collective-permute-start.5 = (f32[8,5,1,8,128]{4,0,3,2,1:T(8,128)}, f32[8,5,1,8,128]{4,0,3,2,1:T(8,128)}, u32[]{:S(2)}, u32[]{:S(2)}) collective-permute-start(f32[8,5,1,8,128]{4,0,3,2,1:T(8,128)} %get-tuple-element.19), channel_id=1, source_target_pairs={{0,1},{1,2},{2,3},{3,4},{4,5},{5,6},{6,7},{7,8},{8,9},{9,10},{10,1... | collective-permute-start | bytes 491528 | tf_op jit(solution)/shard_map/ppermute | solution.py:22
  61.4 17.2 %collective-permute-start.4 = (f32[8,5,1,8,128]{4,0,3,2,1:T(8,128)}, f32[8,5,1,8,128]{4,0,3,2,1:T(8,128)}, u32[]{:S(2)}, u32[]{:S(2)}) collective-permute-start(f32[8,5,1,8,128]{4,0,3,2,1:T(8,128)} %get-tuple-element.20), channel_id=1, source_target_pairs={{1,0},{2,1},{3,2},{4,3},{5,4},{6,5},{7,6},{8,7},{9,8},{10,9},{11,1... | collective-permute-start | bytes 491528 | tf_op jit(solution)/shard_map/ppermute | solution.py:23
  69.7 9.9 %collective-permute-start.2 = (f32[8,5,8,1,128]{4,0,3,2,1:T(8,128)}, f32[8,5,8,1,128]{4,0,3,2,1:T(8,128)}, u32[]{:S(2)}, u32[]{:S(2)}) collective-permute-start(f32[8,5,8,1,128]{4,0,3,2,1:T(8,128)} %get-tuple-element.17), channel_id=1, source_target_pairs={{0,64},{64,128},{128,192},{1,65},{65,129},{129,193},{2,66},{66,130... | collective-permute-start | bytes 491528 | tf_op jit(solution)/shard_map/ppermute | solution.py:22
  71.6 8.3 %collective-permute-start.3 = (f32[8,5,8,1,128]{4,0,3,2,1:T(8,128)}, f32[8,5,8,1,128]{4,0,3,2,1:T(8,128)}, u32[]{:S(2)}, u32[]{:S(2)}) collective-permute-start(f32[8,5,8,1,128]{4,0,3,2,1:T(8,128)} %get-tuple-element.18), channel_id=1, source_target_pairs={{64,0},{128,64},{192,128},{65,1},{129,65},{193,129},{66,2},{130,66... | collective-permute-start | bytes 491528 | tf_op jit(solution)/shard_map/ppermute | solution.py:23
  79.6 4.7 %copy-start.1 = (f32[8,5,8,8,128]{4,0,3,2,1:T(8,128)S(1)}, f32[8,5,8,8,128]{4,0,3,2,1:T(8,128)}, u32[]{:S(2)}) copy-start(f32[8,5,8,8,128]{4,0,3,2,1:T(8,128)} %copy-done) | copy-start | bytes 3932164
  88.9 17.2 %collective-permute-start.9 = (f32[8,5,1,8,128]{4,0,3,2,1:T(8,128)S(1)}, f32[8,5,1,8,128]{4,0,3,2,1:T(8,128)S(1)}, u32[]{:S(2)}, u32[]{:S(2)}) collective-permute-start(f32[8,5,1,8,128]{4,0,3,2,1:T(8,128)S(1)} %get-tuple-element.15), channel_id=1, source_target_pairs={{0,1},{1,2},{2,3},{3,4},{4,5},{5,6},{6,7},{7,8},{8,9},{9,10},{10,1... | collective-permute-start | bytes 491528 | tf_op jit(solution)/shard_map/ppermute | solution.py:22
  90.8 15.3 %collective-permute-start.8 = (f32[8,5,1,8,128]{4,0,3,2,1:T(8,128)S(1)}, f32[8,5,1,8,128]{4,0,3,2,1:T(8,128)S(1)}, u32[]{:S(2)}, u32[]{:S(2)}) collective-permute-start(f32[8,5,1,8,128]{4,0,3,2,1:T(8,128)S(1)} %get-tuple-element.16), channel_id=1, source_target_pairs={{1,0},{2,1},{3,2},{4,3},{5,4},{6,5},{7,6},{8,7},{9,8},{10,9},{11,1... | collective-permute-start | bytes 491528 | tf_op jit(solution)/shard_map/ppermute | solution.py:23
  99.0 8.1 %collective-permute-start.6 = (f32[8,5,8,1,128]{4,0,3,2,1:T(8,128)S(1)}, f32[8,5,8,1,128]{4,0,3,2,1:T(8,128)S(1)}, u32[]{:S(2)}, u32[]{:S(2)}) collective-permute-start(f32[8,5,8,1,128]{4,0,3,2,1:T(8,128)S(1)} %get-tuple-element.13), channel_id=1, source_target_pairs={{0,64},{64,128},{128,192},{1,65},{65,129},{129,193},{2,66},{66,130... | collective-permute-start | bytes 491528 | tf_op jit(solution)/shard_map/ppermute | solution.py:22
  100.9 8.0 %collective-permute-start.7 = (f32[8,5,8,1,128]{4,0,3,2,1:T(8,128)S(1)}, f32[8,5,8,1,128]{4,0,3,2,1:T(8,128)S(1)}, u32[]{:S(2)}, u32[]{:S(2)}) collective-permute-start(f32[8,5,8,1,128]{4,0,3,2,1:T(8,128)S(1)} %get-tuple-element.14), channel_id=1, source_target_pairs={{64,0},{128,64},{192,128},{65,1},{129,65},{193,129},{66,2},{130,66... | collective-permute-start | bytes 491528 | tf_op jit(solution)/shard_map/ppermute | solution.py:23
  114.8 17.4 %collective-permute-start.13 = (f32[8,5,1,8,128]{4,0,3,2,1:T(8,128)S(1)}, f32[8,5,1,8,128]{4,0,3,2,1:T(8,128)S(1)}, u32[]{:S(2)}, u32[]{:S(2)}) collective-permute-start(f32[8,5,1,8,128]{4,0,3,2,1:T(8,128)S(1)} %get-tuple-element.11), channel_id=1, source_target_pairs={{0,1},{1,2},{2,3},{3,4},{4,5},{5,6},{6,7},{7,8},{8,9},{9,10},{10,1... | collective-permute-start | bytes 491528 | tf_op jit(solution)/shard_map/ppermute | solution.py:22
  116.7 15.5 %collective-permute-start.12 = (f32[8,5,1,8,128]{4,0,3,2,1:T(8,128)S(1)}, f32[8,5,1,8,128]{4,0,3,2,1:T(8,128)S(1)}, u32[]{:S(2)}, u32[]{:S(2)}) collective-permute-start(f32[8,5,1,8,128]{4,0,3,2,1:T(8,128)S(1)} %get-tuple-element.12), channel_id=1, source_target_pairs={{1,0},{2,1},{3,2},{4,3},{5,4},{6,5},{7,6},{8,7},{9,8},{10,9},{11,1... | collective-permute-start | bytes 491528 | tf_op jit(solution)/shard_map/ppermute | solution.py:23
  124.9 8.1 %collective-permute-start.10 = (f32[8,5,8,1,128]{4,0,3,2,1:T(8,128)S(1)}, f32[8,5,8,1,128]{4,0,3,2,1:T(8,128)S(1)}, u32[]{:S(2)}, u32[]{:S(2)}) collective-permute-start(f32[8,5,8,1,128]{4,0,3,2,1:T(8,128)S(1)} %get-tuple-element.9), channel_id=1, source_target_pairs={{0,64},{64,128},{128,192},{1,65},{65,129},{129,193},{2,66},{66,130... | collective-permute-start | bytes 491528 | tf_op jit(solution)/shard_map/ppermute | solution.py:22
  126.8 8.0 %collective-permute-start.11 = (f32[8,5,8,1,128]{4,0,3,2,1:T(8,128)S(1)}, f32[8,5,8,1,128]{4,0,3,2,1:T(8,128)S(1)}, u32[]{:S(2)}, u32[]{:S(2)}) collective-permute-start(f32[8,5,8,1,128]{4,0,3,2,1:T(8,128)S(1)} %get-tuple-element.10), channel_id=1, source_target_pairs={{64,0},{128,64},{192,128},{65,1},{129,65},{193,129},{66,2},{130,66... | collective-permute-start | bytes 491528 | tf_op jit(solution)/shard_map/ppermute | solution.py:23
  140.7 17.2 %collective-permute-start.17 = (f32[8,5,1,8,128]{4,0,3,2,1:T(8,128)S(1)}, f32[8,5,1,8,128]{4,0,3,2,1:T(8,128)S(1)}, u32[]{:S(2)}, u32[]{:S(2)}) collective-permute-start(f32[8,5,1,8,128]{4,0,3,2,1:T(8,128)S(1)} %get-tuple-element.7), channel_id=1, source_target_pairs={{0,1},{1,2},{2,3},{3,4},{4,5},{5,6},{6,7},{7,8},{8,9},{9,10},{10,1... | collective-permute-start | bytes 491528 | tf_op jit(solution)/shard_map/ppermute | solution.py:22
  142.6 15.3 %collective-permute-start.16 = (f32[8,5,1,8,128]{4,0,3,2,1:T(8,128)S(1)}, f32[8,5,1,8,128]{4,0,3,2,1:T(8,128)S(1)}, u32[]{:S(2)}, u32[]{:S(2)}) collective-permute-start(f32[8,5,1,8,128]{4,0,3,2,1:T(8,128)S(1)} %get-tuple-element.8), channel_id=1, source_target_pairs={{1,0},{2,1},{3,2},{4,3},{5,4},{6,5},{7,6},{8,7},{9,8},{10,9},{11,1... | collective-permute-start | bytes 491528 | tf_op jit(solution)/shard_map/ppermute | solution.py:23
  150.8 8.1 %collective-permute-start.14 = (f32[8,5,8,1,128]{4,0,3,2,1:T(8,128)S(1)}, f32[8,5,8,1,128]{4,0,3,2,1:T(8,128)S(1)}, u32[]{:S(2)}, u32[]{:S(2)}) collective-permute-start(f32[8,5,8,1,128]{4,0,3,2,1:T(8,128)S(1)} %get-tuple-element.5), channel_id=1, source_target_pairs={{0,64},{64,128},{128,192},{1,65},{65,129},{129,193},{2,66},{66,130... | collective-permute-start | bytes 491528 | tf_op jit(solution)/shard_map/ppermute | solution.py:22
  152.7 8.0 %collective-permute-start.15 = (f32[8,5,8,1,128]{4,0,3,2,1:T(8,128)S(1)}, f32[8,5,8,1,128]{4,0,3,2,1:T(8,128)S(1)}, u32[]{:S(2)}, u32[]{:S(2)}) collective-permute-start(f32[8,5,8,1,128]{4,0,3,2,1:T(8,128)S(1)} %get-tuple-element.6), channel_id=1, source_target_pairs={{64,0},{128,64},{192,128},{65,1},{129,65},{193,129},{66,2},{130,66... | collective-permute-start | bytes 491528 | tf_op jit(solution)/shard_map/ppermute | solution.py:23
where the time goes:
time: 192 us; the launch traced here: 189 us
  starting transfers between devices  91.4 us (48%)
  waiting for transfers between devices  26.7 us (14%)
  other arithmetic  25.2 us (13%)
  blocking collectives  20.3 us (11%)
  local copies, waits for them, and re-layouts  13.6 us (7%)
  matrix products  10.8 us (6%)
    ppermute x8, starting transfers between devices, extended(): lax.ppermute(initial, axis, [(b, a) for a, b in up])  53.7 us
    all_to_all x1, blocking collectives, on_device(): lax.all_to_all(moved_state + update, 'inst', split_axis=0, concat_axis=3,...  20.3 us
    ppermute x8, starting transfers between devices, extended(): lax.ppermute(last, axis, up)  15.4 us
    all_to_all x1, waiting for transfers between devices, on_device(): lax.all_to_all(local_part, 'inst', split_axis=3, concat_axis=0, tiled=True)  14.9 us
    concatenate x4, other arithmetic, extended(): jnp.concatenate([jnp.pad(low, around), shard, jnp.pad(high, around)], axi...  12.9 us
    dot_general x5, matrix products, spectral_term(): product = jnp.dot(matrix, flat, precision=lax.Precision.HIGHEST)  10.8 us
    ppermute x1, starting transfers between devices, extended_2(): after = lax.ppermute(initial, axis, down)  8.23 us
    ppermute x8, waiting for transfers between devices, extended(): lax.ppermute(initial, axis, [(b, a) for a, b in up])  5.55 us
  transfers between devices with their start and end apart: 20, of which 10 were waited for; matrix products, arithmetic and copies ran while one was open for 6% of the time, Pallas kernels for 0%

commit v1 on v0

v1 whole, which is shorter than its diff:
```python
import functools
import math

import jax
import jax.numpy as jnp
from jax import lax
from jax.experimental import pallas as pl
from jax.experimental.pallas import tpu as pltpu
from jax.sharding import PartitionSpec as P

SWEEPS = 4
HALF = math.sqrt(0.5)
MESH = pl.DeviceIdType.MESH


def to_modes(x):
    e = [x[n] + x[n + 4] for n in range(4)]
    o = [x[n] - x[n + 4] for n in range(4)]
    even, odd = e[0] + e[2], e[1] + e[3]
    minus, plus = HALF * (o[1] - o[3]), HALF * (o[1] + o[3])
    return [even + odd, even - odd, o[0] + minus, plus + o[2], e[0] - e[2], e[1] - e[3], o[0] - minus, plus - o[2]]


def from_modes(a):
    even, odd = 0.125 * (a[0] + a[1]), 0.125 * (a[0] - a[1])
    c2, s2 = 0.25 * a[4], 0.25 * a[5]
    e = [even + c2, odd + s2, even - c2, odd - s2]
    c, s = a[2] - a[6], a[3] + a[7]
    o = [0.25 * (a[2] + a[6]), (0.25 * HALF) * (s + c), 0.25 * (a[3] - a[7]), (0.25 * HALF) * (s - c)]
    return [e[n] + o[n] for n in range(4)] + [e[n] - o[n] for n in range(4)]


def kernel(cells, fs_hbm, forcing_hbm, diff_hbm, block_hbm, out_hbm,
           fs, forcing, diff, block, halo, local, fm, rm, neg, u, edge_out, edge_in, back, out,
           load_sem, own_sem, halo_s, halo_r, fs_s, fs_r, part_s, part_r, x_s, x_r, y_s, y_r, back_s, back_r, out_sem):
    i, k = lax.axis_index("inst"), lax.axis_index("cells")
    peers = (i + 1 - 2 * lax.rem(i, 2), lax.rem(i + 2, 4), 3 - i)
    has_left, has_right = k > 0, k < cells - 1
    has_up, has_down = i > 0, i < 3
    own_rows = pl.ds(pl.multiple_of(8 * i, 8), 8)

    loads = [
        pltpu.make_async_copy(fs_hbm, fs, load_sem.at[0]),
        pltpu.make_async_copy(forcing_hbm, forcing, load_sem.at[1]),
        pltpu.make_async_copy(diff_hbm, diff, load_sem.at[2]),
        pltpu.make_async_copy(block_hbm, block, load_sem.at[3]),
        pltpu.make_async_copy(fs_hbm.at[:, :, :, own_rows, :], fm.at[pl.ds(2 * i, 2)], own_sem),
    ]
    for load in loads:
        load.start()

    barrier = pltpu.get_barrier_semaphore()
    for peer in peers:
        pl.semaphore_signal(barrier, inc=1, device_id=(peer, k), device_id_type=MESH)

    @pl.when(has_left)
    def _():
        pl.semaphore_signal(barrier, inc=1, device_id=(i, k - 1), device_id_type=MESH)

    @pl.when(has_right)
    def _():
        pl.semaphore_signal(barrier, inc=1, device_id=(i, k + 1), device_id_type=MESH)

    pl.semaphore_wait(barrier, 3 + has_left.astype(jnp.int32) + has_right.astype(jnp.int32))

    def remote(src, dst, send, recv, device):
        return pltpu.make_async_remote_copy(
            src_ref=src, dst_ref=dst, send_sem=send, recv_sem=recv, device_id=device, device_id_type=MESH)

    def rows_of(peer):
        return pl.ds(pl.multiple_of(8 * peer, 8), 8)

    def fs_copy(x, slot):
        peer = peers[slot]
        return remote(fs.at[:, :, x, rows_of(peer), :], fm.at[pl.ds(2 * i, 2), :, x],
                      fs_s.at[x, slot], fs_r.at[x, slot], (peer, k))

    def part_copy(x, slot):
        peer = peers[slot]
        return remote(local.at[:, :, x, rows_of(peer), :], rm.at[pl.ds(2 * i, 2), :, x],
                      part_s.at[x, slot], part_r.at[x, slot], (peer, k))

    def back_copy(x, slot):
        peer = peers[slot]
        return remote(back.at[peer, x], out.at[:, :, x, own_rows, :],
                      back_s.at[x, slot], back_r.at[x, slot], (peer, k))

    def pair(p):
        return (p, 7 - p)

    def send(copy, p):
        for slot in (1, 2, 0):
            for x in pair(p):
                copy(x, slot).start()

    def arrived(copy, p):
        for slot in range(3):
            for x in pair(p):
                copy(x, slot).wait_recv()

    def fs_edge(side):
        return remote(fs.at[:, :, 7 if side else 0], halo.at[1 - side], halo_s.at[side], halo_r.at[1 - side],
                      (i, k + (1 if side else -1)))

    def x_edge(s, side):
        return remote(u.at[s, 8 if side else 1], u.at[s, 0 if side else 9], x_s.at[s, side], x_r.at[s, 1 - side],
                      (i, k + (1 if side else -1)))

    def y_edge(s, p, side):
        return remote(edge_out.at[s, side, p], edge_in.at[s, 1 - side, p], y_s.at[s, side, p], y_r.at[s, 1 - side, p],
                      (i + (1 if side else -1), k))

    def both(first, second, action):
        pl.when(first)(lambda: action(0))
        pl.when(second)(lambda: action(1))

    loads[0].wait()
    both(has_left, has_right, lambda side: fs_edge(side).start())
    send(fs_copy, 0)
    send(fs_copy, 1)

    def clear(ref, lead):
        zeros = jnp.zeros((8, 128), jnp.float32)

        def body(t, carry):
            ref[(*lead, pl.ds(pl.multiple_of(8 * t, 8), 8), slice(None))] = zeros
            return carry

        lax.fori_loop(0, ref.shape[-2] // 8, body, 0)

    def clear_x(side):
        for n in range(2):
            for v in range(5):
                clear(halo, (side, n, v))
        for s in range(SWEEPS):
            clear(u, (s, 9 if side else 0))

    def clear_y(side):
        for s in range(SWEEPS):
            for p in range(4):
                for t in range(2):
                    clear(edge_in, (s, side, p, t))

    both(jnp.logical_not(has_left), jnp.logical_not(has_right), clear_x)
    both(jnp.logical_not(has_up), jnp.logical_not(has_down), clear_y)

    loads[1].wait()
    loads[2].wait()

    def shifted_sum(c, low, high):
        n = c.shape[0]
        row = lax.broadcasted_iota(jnp.int32, c.shape, 0)
        lane = lax.broadcasted_iota(jnp.int32, c.shape, 1)
        up = jnp.where(row == 0, low, pltpu.roll(c, 1, 0))
        down = jnp.where(row == n - 1, high, pltpu.roll(c, n - 1, 0))
        left = jnp.where(lane == 0, 0.0, pltpu.roll(c, 1, 1))
        right = jnp.where(lane == 127, 0.0, pltpu.roll(c, 127, 1))
        return (up + down) + (left + right)

    def local_plane(x, before, after):
        weight = diff[x]
        for n in range(2):
            for v in range(5):
                c = fs[n, v, x]
                beside = shifted_sum(c, 0.0, 0.0) + (before(n, v) + after(n, v))
                local[n, v, x] = weight * (6.0 * c - beside) - forcing[n, v, x]
        for n in range(2):
            for v in range(5):
                rm[2 * i + n, v, x] = local[n, v, x, own_rows, :]

    def inner(x, carry):
        local_plane(x, lambda n, v: fs[n, v, x - 1], lambda n, v: fs[n, v, x + 1])
        return carry

    lax.fori_loop(1, 7, inner, 0)

    def fs_edge_arrived(side):
        remote(halo.at[side], halo.at[side], halo_s.at[side], halo_r.at[side], (i, k)).wait_recv()

    both(has_left, has_right, fs_edge_arrived)
    local_plane(0, lambda n, v: halo[0, n, v], lambda n, v: fs[n, v, 1])
    local_plane(7, lambda n, v: fs[n, v, 6], lambda n, v: halo[1, n, v])
    send(part_copy, 0)
    send(fs_copy, 2)
    loads[3].wait()
    loads[4].wait()

    def tile(m, v):
        return pl.ds((m * 5 + v) * 8, 8)

    def plane_of(p, t):
        return p + t * (7 - 2 * p)

    def store_edges(s, p, t, x):
        edge_out[s, 0, p, t] = u[s, x + 1, pl.ds(0, 40, stride=8), :]
        edge_out[s, 1, p, t] = u[s, x + 1, pl.ds(7, 40, stride=8), :]

    def apply_block(s, x, m, source):
        for v in range(5):
            total = block[v, 0, x] * source[0]
            for w in range(1, 5):
                total = total + block[v, w, x] * source[w]
            u[s, x + 1, tile(m, v), :] = total

    def first_plane(x):
        for v in range(5):
            f = to_modes([fm[n, v, x] for n in range(8)])
            r = to_modes([rm[n, v, x] for n in range(8)])
            neg[x, tile(0, v), :] = -r[0]
            neg[x, tile(1, v), :] = -r[1]
            for q in range(1, 4):
                neg[x, tile(2 * q, v), :] = -(r[2 * q] + q * f[2 * q + 1])
                neg[x, tile(2 * q + 1, v), :] = q * f[2 * q] - r[2 * q + 1]
        for m in range(8):
            apply_block(0, x, m, [neg[x, tile(m, v), :] for v in range(5)])

    def sweep_plane(s, p, t):
        x = plane_of(p, t)
        weight = diff[x, own_rows, :]
        for q in range(4):
            c = [[u[s - 1, x + 1, tile(2 * q + j, v), :] for v in range(5)] for j in range(2)]
            for j in range(2):
                source = []
                for v in range(5):
                    here = tile(2 * q + j, v)
                    at = (2 * q + j) * 5 + v
                    beside = shifted_sum(c[j][v], edge_in[s - 1, 0, p, t, pl.ds(at, 1), :],
                                         edge_in[s - 1, 1, p, t, pl.ds(at, 1), :])
                    beside = beside + (u[s - 1, x, here, :] + u[s - 1, x + 2, here, :])
                    value = weight * beside + neg[x, here, :]
                    if q:
                        value = value + (float(q) * c[0][v] if j else float(-q) * c[1][v])
                    source.append(value)
                apply_block(s, x, 2 * q + j, source)

    def back_plane(x):
        for v in range(5):
            modes = from_modes([u[SWEEPS, x + 1, tile(m, v), :] for m in range(8)])
            for n in range(8):
                back[n // 2, x, n % 2, v] = fm[n, v, x] + modes[n]
        for n in range(2):
            for v in range(5):
                out[n, v, x, own_rows, :] = back[i, x, n, v]

    def y_arrived(s, p):
        def wait(side):
            remote(edge_in.at[s, side, p], edge_in.at[s, side, p], y_s.at[s, side, p], y_r.at[s, side, p], (i, k)).wait_recv()
        both(has_up, has_down, wait)

    def x_arrived(s):
        def wait(side):
            place = u.at[s, 9 if side else 0]
            remote(place, place, x_s.at[s, side], x_r.at[s, side], (i, k)).wait_recv()
        both(has_left, has_right, wait)

    for d in range(8):
        if d < 4:
            arrived(fs_copy, d)
            arrived(part_copy, d)

            def first(t, carry, d=d):
                x = plane_of(d, t)
                first_plane(x)
                store_edges(0, d, t, x)
                return carry

            lax.fori_loop(0, 2, first, 0)
            both(has_up, has_down, lambda side: y_edge(0, d, side).start())
            if d == 0:
                both(has_left, has_right, lambda side: x_edge(0, side).start())
        for s in range(max(1, d - 3), min(4, d) + 1):
            p = d - s
            y_arrived(s - 1, p)
            if p == 0:
                x_arrived(s - 1)

            def sweep(t, carry, s=s, p=p):
                sweep_plane(s, p, t)
                if s < SWEEPS:
                    store_edges(s, p, t, plane_of(p, t))
                else:
                    back_plane(plane_of(p, t))
                return carry

            lax.fori_loop(0, 2, sweep, 0)
            if s < SWEEPS:
                both(has_up, has_down, lambda side: y_edge(s, p, side).start())
                if p == 0:
                    both(has_left, has_right, lambda side: x_edge(s, side).start())
            else:
                send(back_copy, p)
        if d == 0:
            send(part_copy, 1)
            send(fs_copy, 3)
        if d == 1:
            send(part_copy, 2)
            send(part_copy, 3)

    writes = []
    for p in range(4):
        arrived(back_copy, p)
        for x in pair(p):
            write = pltpu.make_async_copy(out.at[:, :, x], out_hbm.at[:, :, x], out_sem.at[x])
            write.start()
            writes.append(write)

    both(has_left, has_right, lambda side: fs_edge(side).wait_send())
    for s in range(SWEEPS):
        both(has_left, has_right, lambda side: x_edge(s, side).wait_send())
        for p in range(4):
            both(has_up, has_down, lambda side: y_edge(s, p, side).wait_send())
    for copy in (fs_copy, part_copy, back_copy):
        for x in range(8):
            for slot in range(3):
                copy(x, slot).wait_send()
    for write in writes:
        write.wait()


def on_device(cells, flow_state, forcing, diffusion, block_inverse):
    f32 = jnp.float32
    dma = pltpu.SemaphoreType.DMA
    any_spec = pl.BlockSpec(memory_space=pl.ANY)
    return pl.pallas_call(
        functools.partial(kernel, cells),
        out_shape=jax.ShapeDtypeStruct(flow_state.shape, f32),
        in_specs=[any_spec] * 4,
        out_specs=any_spec,
        scratch_shapes=[
            pltpu.VMEM((2, 5, 8, 32, 128), f32),
            pltpu.VMEM((2, 5, 8, 32, 128), f32),
            pltpu.VMEM((8, 32, 128), f32),
            pltpu.VMEM((5, 5, 8, 8, 128), f32),
            pltpu.VMEM((2, 2, 5, 32, 128), f32),
            pltpu.VMEM((2, 5, 8, 32, 128), f32),
            pltpu.VMEM((8, 5, 8, 8, 128), f32),
            pltpu.VMEM((8, 5, 8, 8, 128), f32),
            pltpu.VMEM((8, 320, 128), f32),
            pltpu.VMEM((SWEEPS + 1, 10, 320, 128), f32),
            pltpu.VMEM((SWEEPS, 2, 4, 2, 40, 128), f32),
            pltpu.VMEM((SWEEPS, 2, 4, 2, 40, 128), f32),
            pltpu.VMEM((4, 8, 2, 5, 8, 128), f32),
            pltpu.VMEM((2, 5, 8, 32, 128), f32),
            dma((4,)),
            dma(()),
            dma((2,)), dma((2,)),
            dma((8, 3)), dma((8, 3)),
            dma((8, 3)), dma((8, 3)),
            dma((SWEEPS, 2)), dma((SWEEPS, 2)),
            dma((SWEEPS, 2, 4)), dma((SWEEPS, 2, 4)),
            dma((8, 3)), dma((8, 3)),
            dma((8,)),
        ],
        compiler_params=pltpu.CompilerParams(
            collective_id=0, has_side_effects=True, vmem_limit_bytes=56 * 1024 * 1024),
        name="update",
    )(flow_state, forcing, diffusion, block_inverse)


def solution(mesh):
    in_specs = (
        P("inst", None, "cells", None, None),
        P("inst", None, "cells", None, None),
        P("cells", None, None),
        P(None, None, "cells", "inst", None),
    )
    out_specs = P("inst", None, "cells", None, None)
    return jax.shard_map(
        functools.partial(on_device, mesh.shape["cells"]),
        mesh=mesh, in_specs=in_specs, out_specs=out_specs, check_vma=False,
    )
```

time: 192 us -> 82.7 us (0.43)
  the two profiles are of different devices: /device:TPU:24 before, /device:TPU:1 now
where the time goes in v1:
time: 82.7 us; the launch traced here: 82.6 us
  Pallas kernels  80.2 us (97%)
  local copies, waits for them, and re-layouts  2.47 us (3%)
    pallas_call x1, Pallas kernels, on_device(): pl.pallas_call(functools.partial(kernel, cells), out_shape=jax.ShapeDtype...  80.2 us
    unnamed x1, local copies, waits for them, and re-layouts  2.47 us

profile of v1, /device:TPU:1, one launch (start us, length us, event | category | flops | bytes accessed | tf_op | source)
XLA Modules:
  0.0 82.6 jit_solution(7947194593300373033)
XLA Ops:
  0.0 80.2 %update.1 = f32[2,5,8,32,128]{4,3,2,1,0:T(8,128)} custom-call(f32[2,5,8,32,128]{4,3,2,1,0:T(8,128)} %fs_hbm.1, f32[2,5,8,32,128]{4,3,2,1,0:T(8,128)} %forcing_hbm.1, f32[8,32,128]{2,1,0:T(8,128)} %diff_hbm.1, f32[5,5,8,8,128]{4,3,2,1,0:T(8,128)} %block_hbm.1), custom_call_target="tpu_custom_call" | custom-call | tf_op jit(solution)/shard_map/update/pallas_call | solution.py:324
  80.2 2.5 %copy.6 = f32[2,5,8,32,128]{4,3,2,1,0:T(8,128)} copy(f32[2,5,8,32,128]{4,3,2,1,0:T(8,128)} %update.1) | data formatting | bytes 2621440

commit v2 on v1

--- a/solution.py
+++ b/solution.py
@@ -9,6 +9,8 @@
 from jax.sharding import PartitionSpec as P
 
 SWEEPS = 4
+CUT = 32
+PIECES = 4
 HALF = math.sqrt(0.5)
 MESH = pl.DeviceIdType.MESH
 
@@ -30,13 +32,18 @@
     return [e[n] + o[n] for n in range(4)] + [e[n] - o[n] for n in range(4)]
 
 
-def kernel(cells, fs_hbm, forcing_hbm, diff_hbm, block_hbm, out_hbm,
-           fs, forcing, diff, block, halo, local, fm, rm, neg, u, edge_out, edge_in, back, out,
-           load_sem, own_sem, halo_s, halo_r, fs_s, fs_r, part_s, part_r, x_s, x_r, y_s, y_r, back_s, back_r, out_sem):
+def kernel(cells, fs_hbm, forcing_hbm, diff_hbm, block_hbm, out,
+           fs, forcing, diff, block, halo, local, fm, rm, neg, u, edge_out, edge_in, back, relay_fs, relay_u,
+           load_sem, sent, halo_r, fs_r, part_r, x_r, y_r, back_r, relay_r):
     i, k = lax.axis_index("inst"), lax.axis_index("cells")
     peers = (i + 1 - 2 * lax.rem(i, 2), lax.rem(i + 2, 4), 3 - i)
     has_left, has_right = k > 0, k < cells - 1
     has_up, has_down = i > 0, i < 3
+    direct_left, direct_right = has_left & (k != CUT), has_right & (k != CUT - 1)
+    column, upper = lax.rem(k, CUT), k // CUT
+    ways = (None, CUT - 1 - (CUT - 1) * (1 - upper), 7, 24)
+    piece = sum(jnp.where(column == at, n, 0) for n, at in enumerate(ways) if n)
+    relays = piece > 0
     own_rows = pl.ds(pl.multiple_of(8 * i, 8), 8)
 
     loads = [
@@ -44,7 +51,7 @@
         pltpu.make_async_copy(forcing_hbm, forcing, load_sem.at[1]),
         pltpu.make_async_copy(diff_hbm, diff, load_sem.at[2]),
         pltpu.make_async_copy(block_hbm, block, load_sem.at[3]),
-        pltpu.make_async_copy(fs_hbm.at[:, :, :, own_rows, :], fm.at[pl.ds(2 * i, 2)], own_sem),
+        pltpu.make_async_copy(fs_hbm.at[:, :, :, own_rows, :], fm.at[pl.ds(2 * i, 2)], load_sem.at[4]),
     ]
     for load in loads:
         load.start()
@@ -53,15 +60,22 @@
     for peer in peers:
         pl.semaphore_signal(barrier, inc=1, device_id=(peer, k), device_id_type=MESH)
 
-    @pl.when(has_left)
+    def greet(target):
+        pl.semaphore_signal(barrier, inc=1, device_id=(i, target), device_id_type=MESH)
+
+    pl.when(direct_left)(lambda: greet(k - 1))
+    pl.when(direct_right)(lambda: greet(k + 1))
+    pl.when(relays)(lambda: greet(CUT - upper))
+
+    @pl.when((k == CUT - 1) | (k == CUT))
     def _():
-        pl.semaphore_signal(barrier, inc=1, device_id=(i, k - 1), device_id_type=MESH)
-
-    @pl.when(has_right)
-    def _():
-        pl.semaphore_signal(barrier, inc=1, device_id=(i, k + 1), device_id_type=MESH)
-
-    pl.semaphore_wait(barrier, 3 + has_left.astype(jnp.int32) + has_right.astype(jnp.int32))
+        for at in (upper * (2 * CUT - 1), upper * CUT + 7, upper * CUT + 24):
+            greet(at)
+        greet(CUT - upper)
+
+    count = 3 + sum(jnp.where(held, n, 0) for held, n in (
+        (direct_left, 1), (direct_right, 1), (relays, 1), ((k == CUT - 1) | (k == CUT), PIECES)))
+    pl.semaphore_wait(barrier, count)
 
     def remote(src, dst, send, recv, device):
         return pltpu.make_async_remote_copy(
@@ -73,17 +87,17 @@
     def fs_copy(x, slot):
         peer = peers[slot]
         return remote(fs.at[:, :, x, rows_of(peer), :], fm.at[pl.ds(2 * i, 2), :, x],
-                      fs_s.at[x, slot], fs_r.at[x, slot], (peer, k))
+                      sent.at[0], fs_r.at[min(x, 7 - x)], (peer, k))
 
     def part_copy(x, slot):
         peer = peers[slot]
         return remote(local.at[:, :, x, rows_of(peer), :], rm.at[pl.ds(2 * i, 2), :, x],
-                      part_s.at[x, slot], part_r.at[x, slot], (peer, k))
+                      sent.at[1], part_r.at[min(x, 7 - x)], (peer, k))
 
     def back_copy(x, slot):
         peer = peers[slot]
         return remote(back.at[peer, x], out.at[:, :, x, own_rows, :],
-                      back_s.at[x, slot], back_r.at[x, slot], (peer, k))
+                      sent.at[2], back_r.at[min(x, 7 - x)], (peer, k))
 
     def pair(p):
         return (p, 7 - p)
@@ -93,21 +107,67 @@
             for x in pair(p):
                 copy(x, slot).start()
 
-    def arrived(copy, p):
-        for slot in range(3):
-            for x in pair(p):
-                copy(x, slot).wait_recv()
-
-    def fs_edge(side):
-        return remote(fs.at[:, :, 7 if side else 0], halo.at[1 - side], halo_s.at[side], halo_r.at[1 - side],
-                      (i, k + (1 if side else -1)))
-
-    def x_edge(s, side):
-        return remote(u.at[s, 8 if side else 1], u.at[s, 0 if side else 9], x_s.at[s, side], x_r.at[s, 1 - side],
-                      (i, k + (1 if side else -1)))
+    def await_bytes(ref, sem):
+        remote(ref, ref, sem, sem, (i, k)).wait_recv()
+
+    six = fm.at[pl.ds(0, 6), :, pl.ds(0, 2)]
+
+    pieces = range(PIECES)
+
+    def fs_piece(ref, n, lead):
+        return ref.at[n // 2, :, lead, pl.ds(16 * (n % 2), 16), :]
+
+    def halo_piece(side, n):
+        return halo.at[side, n // 2, :, pl.ds(16 * (n % 2), 16), :]
+
+    def u_piece(s, x, n):
+        return u.at[s, x, pl.ds(80 * n, 80), :]
+
+    def fs_edge(side, n):
+        return remote(fs_piece(fs, n, 7 if side else 0), halo_piece(1 - side, n),
+                      sent.at[5 + side], halo_r.at[1 - side], (i, k + (1 if side else -1)))
+
+    def x_edge(s, side, n):
+        return remote(u_piece(s, 8 if side else 1, n), u_piece(s, 0 if side else 9, n),
+                      sent.at[3 + side], x_r.at[s, 1 - side], (i, k + (1 if side else -1)))
+
+    def way(side, n):
+        return (i, (2 * CUT - 1, CUT + 7, CUT + 24)[n - 1] if side else (0, 7, 24)[n - 1])
+
+    def fs_far(side, n):
+        return remote(fs_piece(fs, n, 7 if side else 0), relay_fs, sent.at[5 + side], relay_r.at[SWEEPS], way(side, n))
+
+    def x_far(s, side, n):
+        return remote(u_piece(s, 8 if side else 1, n), relay_u.at[s], sent.at[3 + side], relay_r.at[s], way(side, n))
+
+    def fs_relayed():
+        target = halo.at[1 - upper, piece // 2, :, pl.ds(pl.multiple_of(16 * lax.rem(piece, 2), 16), 16), :]
+        return remote(relay_fs, target, sent.at[10], halo_r.at[1 - upper], (i, CUT - 1 + upper))
+
+    def x_relayed(s):
+        target = u.at[s, 9 - 9 * upper, pl.ds(pl.multiple_of(80 * piece, 8), 80), :]
+        return remote(relay_u.at[s], target, sent.at[9], x_r.at[s, 1 - upper], (i, CUT - 1 + upper))
+
+    def send_edge(near, far, side):
+        @pl.when(direct_right if side else direct_left)
+        def _():
+            for n in pieces:
+                near(side, n).start()
+
+        @pl.when(k == (CUT - 1 if side else CUT))
+        def _():
+            for n in pieces[1:]:
+                far(side, n).start()
+            near(side, 0).start()
+
+    def relay(event, copy, buffer):
+        @pl.when(relays)
+        def _():
+            await_bytes(buffer, relay_r.at[event])
+            copy().start()
 
     def y_edge(s, p, side):
-        return remote(edge_out.at[s, side, p], edge_in.at[s, 1 - side, p], y_s.at[s, side, p], y_r.at[s, 1 - side, p],
+        return remote(edge_out.at[s, side, p], edge_in.at[s, 1 - side, p], sent.at[7 + side], y_r.at[s, 1 - side, p],
                       (i + (1 if side else -1), k))
 
     def both(first, second, action):
@@ -115,7 +175,8 @@
         pl.when(second)(lambda: action(1))
 
     loads[0].wait()
-    both(has_left, has_right, lambda side: fs_edge(side).start())
+    for side in range(2):
+        send_edge(fs_edge, fs_far, side)
     send(fs_copy, 0)
     send(fs_copy, 1)
 
@@ -174,10 +235,10 @@
 
     lax.fori_loop(1, 7, inner, 0)
 
-    def fs_edge_arrived(side):
-        remote(halo.at[side], halo.at[side], halo_s.at[side], halo_r.at[side], (i, k)).wait_recv()
-
-    both(has_left, has_right, fs_edge_arrived)
+    send(part_copy, 1)
+    relay(SWEEPS, fs_relayed, relay_fs)
+
+    both(has_left, has_right, lambda side: await_bytes(halo.at[side], halo_r.at[side]))
     local_plane(0, lambda n, v: halo[0, n, v], lambda n, v: fs[n, v, 1])
     local_plane(7, lambda n, v: fs[n, v, 6], lambda n, v: halo[1, n, v])
     send(part_copy, 0)
@@ -243,89 +304,98 @@
                 out[n, v, x, own_rows, :] = back[i, x, n, v]
 
     def y_arrived(s, p):
-        def wait(side):
-            remote(edge_in.at[s, side, p], edge_in.at[s, side, p], y_s.at[s, side, p], y_r.at[s, side, p], (i, k)).wait_recv()
-        both(has_up, has_down, wait)
+        both(has_up, has_down, lambda side: await_bytes(edge_in.at[s, side, p], y_r.at[s, side, p]))
 
     def x_arrived(s):
-        def wait(side):
-            place = u.at[s, 9 if side else 0]
-            remote(place, place, x_s.at[s, side], x_r.at[s, side], (i, k)).wait_recv()
-        both(has_left, has_right, wait)
+        both(has_left, has_right, lambda side: await_bytes(u.at[s, 9 if side else 0], x_r.at[s, side]))
+
+    def send_x(s, side):
+        send_edge(functools.partial(x_edge, s), functools.partial(x_far, s), side)
+
+    def run(s, p, body):
+        def one(t, carry):
+            body(t)
+            if s < SWEEPS:
+                store_edges(s, p, t, plane_of(p, t))
+            return carry
+
+        if p == 0 and s < SWEEPS:
+            for t in range(2):
+                one(t, 0)
+                send_x(s, t)
+        else:
+            lax.fori_loop(0, 2, one, 0)
+        if s < SWEEPS:
+            both(has_up, has_down, lambda side: y_edge(s, p, side).start())
 
     for d in range(8):
-        if d < 4:
-            arrived(fs_copy, d)
-            arrived(part_copy, d)
-
-            def first(t, carry, d=d):
-                x = plane_of(d, t)
-                first_plane(x)
-                store_edges(0, d, t, x)
-                return carry
-
-            lax.fori_loop(0, 2, first, 0)
-            both(has_up, has_down, lambda side: y_edge(0, d, side).start())
-            if d == 0:
-                both(has_left, has_right, lambda side: x_edge(0, side).start())
+        for p in ((0, 1), (), (2,), (3,), (), (), (), ())[d]:
+            await_bytes(six, fs_r.at[p])
+            await_bytes(six, part_r.at[p])
+            run(0, p, lambda t: first_plane(plane_of(p, t)))
+        if d == 0:
+            send(part_copy, 2)
+            send(fs_copy, 3)
         for s in range(max(1, d - 3), min(4, d) + 1):
             p = d - s
             y_arrived(s - 1, p)
             if p == 0:
+                if s == SWEEPS:
+                    relay(s - 1, functools.partial(x_relayed, s - 1), relay_u.at[s - 1])
                 x_arrived(s - 1)
 
-            def sweep(t, carry, s=s, p=p):
+            def sweep(t):
                 sweep_plane(s, p, t)
-                if s < SWEEPS:
-                    store_edges(s, p, t, plane_of(p, t))
-                else:
+                if s == SWEEPS:
                     back_plane(plane_of(p, t))
-                return carry
-
-            lax.fori_loop(0, 2, sweep, 0)
-            if s < SWEEPS:
-                both(has_up, has_down, lambda side: y_edge(s, p, side).start())
-                if p == 0:
-                    both(has_left, has_right, lambda side: x_edge(s, side).start())
-            else:
+
+            run(s, p, sweep)
+            if s == SWEEPS:
                 send(back_copy, p)
-        if d == 0:
-            send(part_copy, 1)
-            send(fs_copy, 3)
         if d == 1:
-            send(part_copy, 2)
             send(part_copy, 3)
-
-    writes = []
+        if d < SWEEPS - 1:
+            relay(d, functools.partial(x_relayed, d), relay_u.at[d])
+
     for p in range(4):
-        arrived(back_copy, p)
-        for x in pair(p):
-            write = pltpu.make_async_copy(out.at[:, :, x], out_hbm.at[:, :, x], out_sem.at[x])
-            write.start()
-            writes.append(write)
-
-    both(has_left, has_right, lambda side: fs_edge(side).wait_send())
-    for s in range(SWEEPS):
-        both(has_left, has_right, lambda side: x_edge(s, side).wait_send())
-        for p in range(4):
-            both(has_up, has_down, lambda side: y_edge(s, p, side).wait_send())
-    for copy in (fs_copy, part_copy, back_copy):
-        for x in range(8):
-            for slot in range(3):
-                copy(x, slot).wait_send()
-    for write in writes:
-        write.wait()
+        await_bytes(six, back_r.at[p])
+
+    def done(ref, sem):
+        remote(ref, ref, sem, sem, (i, k)).wait_send()
+
+    for n in range(3):
+        done(fs.at[:, :, pl.ds(0, 6)], sent.at[n])
+
+    def edges_done(side):
+        done(u.at[pl.ds(0, SWEEPS), 1], sent.at[3 + side])
+        done(halo.at[side], sent.at[5 + side])
+
+    both(has_left, has_right, edges_done)
+    both(has_up, has_down, lambda side: done(edge_out.at[:, side], sent.at[7 + side]))
+
+    @pl.when(relays)
+    def _():
+        done(relay_u, sent.at[9])
+        done(relay_fs, sent.at[10])
+
+
+def store(source, target, sem):
+    copies = [pltpu.make_async_copy(source.at[:, :, x], target.at[:, :, x], sem.at[x]) for x in range(8)]
+    for copy in copies:
+        copy.start()
+    for copy in copies:
+        copy.wait()
 
 
 def on_device(cells, flow_state, forcing, diffusion, block_inverse):
     f32 = jnp.float32
     dma = pltpu.SemaphoreType.DMA
     any_spec = pl.BlockSpec(memory_space=pl.ANY)
-    return pl.pallas_call(
+    moved = pl.pallas_call(
         functools.partial(kernel, cells),
-        out_shape=jax.ShapeDtypeStruct(flow_state.shape, f32),
+        out_shape=pltpu.VMEM(flow_state.shape, f32),
         in_specs=[any_spec] * 4,
-        out_specs=any_spec,
+        out_specs=pl.BlockSpec(memory_space=pltpu.VMEM),
         scratch_shapes=[
             pltpu.VMEM((2, 5, 8, 32, 128), f32),
             pltpu.VMEM((2, 5, 8, 32, 128), f32),
@@ -340,21 +410,20 @@
             pltpu.VMEM((SWEEPS, 2, 4, 2, 40, 128), f32),
             pltpu.VMEM((SWEEPS, 2, 4, 2, 40, 128), f32),
             pltpu.VMEM((4, 8, 2, 5, 8, 128), f32),
-            pltpu.VMEM((2, 5, 8, 32, 128), f32),
-            dma((4,)),
-            dma(()),
-            dma((2,)), dma((2,)),
-            dma((8, 3)), dma((8, 3)),
-            dma((8, 3)), dma((8, 3)),
-            dma((SWEEPS, 2)), dma((SWEEPS, 2)),
-            dma((SWEEPS, 2, 4)), dma((SWEEPS, 2, 4)),
-            dma((8, 3)), dma((8, 3)),
-            dma((8,)),
+            pltpu.VMEM((5, 16, 128), f32),
+            pltpu.VMEM((SWEEPS, 80, 128), f32),
+            dma((5,)),
+            dma((11,)),
+            dma((2,)), dma((4,)), dma((4,)), dma((SWEEPS, 2)), dma((SWEEPS, 2, 4)), dma((4,)), dma((SWEEPS + 1,)),
         ],
         compiler_params=pltpu.CompilerParams(
-            collective_id=0, has_side_effects=True, vmem_limit_bytes=56 * 1024 * 1024),
+            collective_id=0, has_side_effects=True, vmem_limit_bytes=65640448),
         name="update",
     )(flow_state, forcing, diffusion, block_inverse)
+    return pl.pallas_call(
+        store, out_shape=jax.ShapeDtypeStruct(flow_state.shape, f32), in_specs=[any_spec], out_specs=any_spec,
+        scratch_shapes=[dma((8,))], compiler_params=pltpu.CompilerParams(vmem_limit_bytes=8 * 1024 * 1024), name="store",
+    )(moved)
 
 
 def solution(mesh):

time: 82.7 us -> 77.9 us (0.942)
  the two profiles are of different devices: /device:TPU:1 before, /device:TPU:24 now
where the time goes in v2:
time: 77.9 us; the launch traced here: 77.8 us
  Pallas kernels  77.8 us (100%)
    pallas_call x1, Pallas kernels, on_device(): pl.pallas_call(functools.partial(kernel, cells), out_shape=pltpu.VMEM(flo...  76.7 us

profile of v2, /device:TPU:24, one launch (start us, length us, event | category | flops | bytes accessed | tf_op | source)
XLA Modules:
  0.0 77.8 jit_solution(7319510712042600107)
XLA Ops:
  0.0 76.7 %update.1.source = f32[2,5,8,32,128]{4,3,2,1,0:T(8,128)S(1)} custom-call(f32[2,5,8,32,128]{4,3,2,1,0:T(8,128)} %fs_hbm.1, f32[2,5,8,32,128]{4,3,2,1,0:T(8,128)} %forcing_hbm.1, f32[8,32,128]{2,1,0:T(8,128)} %diff_hbm.1, f32[5,5,8,8,128]{4,3,2,1,0:T(8,128)} %block_hbm.1), custom_call_target="tpu_custom_call" | custom-call | tf_op jit(solution)/shard_map/update/pallas_call | solution.py:394
  76.7 1.1 %store.1 = f32[2,5,8,32,128]{4,3,2,1,0:T(8,128)} custom-call(f32[2,5,8,32,128]{4,3,2,1,0:T(8,128)S(1)} %update.1.source), custom_call_target="tpu_custom_call" | custom-call | tf_op jit(solution)/shard_map/store/pallas_call | solution.py:423

commit v3 on v2

--- a/solution.py
+++ b/solution.py
@@ -11,6 +11,7 @@
 SWEEPS = 4
 CUT = 32
 PIECES = 4
+RELAYED = 2
 HALF = math.sqrt(0.5)
 MESH = pl.DeviceIdType.MESH
 
@@ -41,8 +42,8 @@
     has_up, has_down = i > 0, i < 3
     direct_left, direct_right = has_left & (k != CUT), has_right & (k != CUT - 1)
     column, upper = lax.rem(k, CUT), k // CUT
-    ways = (None, CUT - 1 - (CUT - 1) * (1 - upper), 7, 24)
-    piece = sum(jnp.where(column == at, n, 0) for n, at in enumerate(ways) if n)
+    ways = (None, None, 7, 24)
+    piece = sum(jnp.where(column == at, n, 0) for n, at in enumerate(ways) if at)
     relays = piece > 0
     own_rows = pl.ds(pl.multiple_of(8 * i, 8), 8)
 
@@ -69,12 +70,13 @@
 
     @pl.when((k == CUT - 1) | (k == CUT))
     def _():
-        for at in (upper * (2 * CUT - 1), upper * CUT + 7, upper * CUT + 24):
-            greet(at)
+        for at in ways:
+            if at is not None:
+                greet(upper * CUT + at)
         greet(CUT - upper)
 
     count = 3 + sum(jnp.where(held, n, 0) for held, n in (
-        (direct_left, 1), (direct_right, 1), (relays, 1), ((k == CUT - 1) | (k == CUT), PIECES)))
+        (direct_left, 1), (direct_right, 1), (relays, 1), ((k == CUT - 1) | (k == CUT), 1 + sum(at is not None for at in ways))))
     pl.semaphore_wait(barrier, count)
 
     def remote(src, dst, send, recv, device):
@@ -132,7 +134,7 @@
                       sent.at[3 + side], x_r.at[s, 1 - side], (i, k + (1 if side else -1)))
 
     def way(side, n):
-        return (i, (2 * CUT - 1, CUT + 7, CUT + 24)[n - 1] if side else (0, 7, 24)[n - 1])
+        return (i, CUT * side + ways[n])
 
     def fs_far(side, n):
         return remote(fs_piece(fs, n, 7 if side else 0), relay_fs, sent.at[5 + side], relay_r.at[SWEEPS], way(side, n))
@@ -156,9 +158,8 @@
 
         @pl.when(k == (CUT - 1 if side else CUT))
         def _():
-            for n in pieces[1:]:
-                far(side, n).start()
-            near(side, 0).start()
+            for n in pieces:
+                (near if ways[n] is None else far)(side, n).start()
 
     def relay(event, copy, buffer):
         @pl.when(relays)
@@ -235,13 +236,13 @@
 
     lax.fori_loop(1, 7, inner, 0)
 
-    send(part_copy, 1)
     relay(SWEEPS, fs_relayed, relay_fs)
 
     both(has_left, has_right, lambda side: await_bytes(halo.at[side], halo_r.at[side]))
     local_plane(0, lambda n, v: halo[0, n, v], lambda n, v: fs[n, v, 1])
     local_plane(7, lambda n, v: fs[n, v, 6], lambda n, v: halo[1, n, v])
     send(part_copy, 0)
+    send(part_copy, 1)
     send(fs_copy, 2)
     loads[3].wait()
     loads[4].wait()
@@ -310,7 +311,8 @@
         both(has_left, has_right, lambda side: await_bytes(u.at[s, 9 if side else 0], x_r.at[s, side]))
 
     def send_x(s, side):
-        send_edge(functools.partial(x_edge, s), functools.partial(x_far, s), side)
+        near = functools.partial(x_edge, s)
+        send_edge(near, functools.partial(x_far, s) if s < RELAYED else near, side)
 
     def run(s, p, body):
         def one(t, carry):
@@ -340,8 +342,6 @@
             p = d - s
             y_arrived(s - 1, p)
             if p == 0:
-                if s == SWEEPS:
-                    relay(s - 1, functools.partial(x_relayed, s - 1), relay_u.at[s - 1])
                 x_arrived(s - 1)
 
             def sweep(t):
@@ -354,7 +354,7 @@
                 send(back_copy, p)
         if d == 1:
             send(part_copy, 3)
-        if d < SWEEPS - 1:
+        if d < RELAYED:
             relay(d, functools.partial(x_relayed, d), relay_u.at[d])
 
     for p in range(4):
@@ -375,7 +375,7 @@
 
     @pl.when(relays)
     def _():
-        done(relay_u, sent.at[9])
+        done(relay_u.at[pl.ds(0, RELAYED)], sent.at[9])
         done(relay_fs, sent.at[10])
 
 

time: 77.9 us -> 73.8 us (0.947)
  Pallas kernels: 77.8 us -> 73.4 us
    pallas_call x1, Pallas kernels: 76.7 us -> 72.2 us  [on_device(): pl.pallas_call(functools.partial(kernel, cells), out_shape=pltpu.VMEM(flo...]
where the time goes in v3:
time: 73.8 us; the launch traced here: 73.4 us
  Pallas kernels  73.4 us (99%)
    pallas_call x1, Pallas kernels, on_device(): pl.pallas_call(functools.partial(kernel, cells), out_shape=pltpu.VMEM(flo...  72.2 us

profile of v3, /device:TPU:24, one launch (start us, length us, event | category | flops | bytes accessed | tf_op | source)
XLA Modules:
  0.0 73.4 jit_solution(15825223635335106763)
XLA Ops:
  0.0 72.2 %update.1.source = f32[2,5,8,32,128]{4,3,2,1,0:T(8,128)S(1)} custom-call(f32[2,5,8,32,128]{4,3,2,1,0:T(8,128)} %fs_hbm.1, f32[2,5,8,32,128]{4,3,2,1,0:T(8,128)} %forcing_hbm.1, f32[8,32,128]{2,1,0:T(8,128)} %diff_hbm.1, f32[5,5,8,8,128]{4,3,2,1,0:T(8,128)} %block_hbm.1), custom_call_target="tpu_custom_call" | custom-call | tf_op jit(solution)/shard_map/update/pallas_call | solution.py:394
  72.3 1.1 %store.1 = f32[2,5,8,32,128]{4,3,2,1,0:T(8,128)} custom-call(f32[2,5,8,32,128]{4,3,2,1,0:T(8,128)S(1)} %update.1.source), custom_call_target="tpu_custom_call" | custom-call | tf_op jit(solution)/shard_map/store/pallas_call | solution.py:423
